TPU v7x, 128 devices: a whole 4x4x4 slice. The times are simulated.
128 devices in a mesh: blk: 8 (over z, y_hi), rows: 16 (over x, y_lo, core).
Axes of the slice: x: 4, y: 4 (y_hi: 2, y_lo: 2; y = y_hi * 2 + y_lo), z: 4, core: 2. Of those that a mesh axis runs over, the one named last changes fastest.
Arguments:
- embeddings: bfloat16 [65536, 768], P(('blk', 'rows')), as said below
- centroids: bfloat16 [8192, 768], P('blk'), as said below
- log_mix: float32 [8192], P('blk'), may hold values from -1.5 to 3.7
Outputs:
- new_centroids: float32 [8192, 768], P('blk')
- new_weights: float32 [8192], P('blk')
Inputs may be any that keep to these rules, and one draw needn't show every extreme that they name: `embeddings`: real vectors of no fixed length. `centroids`: real vectors of no fixed length.
All inputs are finite; a program needn't handle non-finite values.
Results may differ from a plain program's by a relative error of at most 0.0024.
Values may be sent and summed in bfloat16 or wider, within the bound.
A program may use at most 64 MiB of HBM per device.

v0:
```python
import math

import jax
import jax.numpy as jnp
from jax import lax
from jax.sharding import PartitionSpec as P

K = 8192


concentration = 32.0


def sent_to_all(x, axis):
    count = lax.axis_size(axis)
    return lax.all_to_all(jnp.broadcast_to(x[None], (count, *x.shape)), axis, 0, 0, tiled=True)


def of_everyone(x, axis):
    everything = sent_to_all(x, axis)
    return jnp.sum(everything, axis=0)


def split_up(x, dim, count):
    lengths = x.shape
    pieces = x.reshape(*lengths[:dim], count, lengths[dim] // count, *lengths[dim + 1 :])
    return jnp.moveaxis(pieces, dim, 0)


def summed_on_arrival(x, axis, dim):
    pieces = split_up(x, dim, lax.axis_size(axis))
    arrived = lax.all_to_all(pieces, axis, split_axis=0, concat_axis=0, tiled=True)
    return arrived.sum(axis=0)


def side_by_side(arrays, axis, dim, along):
    widths = [math.prod(a.shape[along:]) for a in arrays]
    both = jnp.concatenate(
        [a.reshape(*a.shape[:along], w) for a, w in zip(arrays, widths)], axis=along
    )
    filled = summed_on_arrival(both, axis, dim)
    pieces = jnp.split(filled, [sum(widths[:k]) for k in range(1, len(widths))], axis=along)
    return tuple(
        (b.reshape(*filled.shape[:along], *a.shape[along:]) for a, b in zip(arrays, pieces))
    )


def side_by_side_2(arrays, axis, dim, along):
    widths = [math.prod(a.shape[along:]) for a in arrays]
    both = jnp.concatenate(
        [a.reshape(*a.shape[:along], w) for a, w in zip(arrays, widths)], axis=along
    )
    filled = lax.all_gather(both, axis, axis=dim, tiled=True)
    pieces = jnp.split(filled, [sum(widths[:k]) for k in range(1, len(widths))], axis=along)
    return tuple(
        (b.reshape(*filled.shape[:along], *a.shape[along:]) for a, b in zip(arrays, pieces))
    )


def to_unit(values):
    values = values.astype(jnp.float32)
    return (values * lax.rsqrt(jnp.sum(values * values, axis=-1, keepdims=True) + 1e-06)).astype(
        jnp.bfloat16
    )


def finish(weighted, masses, factor):
    new_centroids = weighted * lax.rsqrt(
        jnp.sum(weighted * weighted, axis=1, keepdims=True) + 1e-06
    )
    return (new_centroids, masses * factor)


def local(embeddings, centroids, log_mix):
    centroid_units = to_unit(centroids)
    row_units = to_unit(embeddings)
    gathered = lax.all_gather(row_units, "blk", axis=0, tiled=True)
    row_total = gathered.shape[0]
    block_rows = math.gcd(row_total, 512)
    grouped = gathered.reshape(row_total // block_rows, block_rows, gathered.shape[1])

    def exponents(row_block):
        cosines = lax.dot_general(
            row_block, centroid_units, (((1,), (1,)), ((), ())), preferred_element_type=jnp.float32
        )
        return jnp.exp(log_mix[None, :] + concentration * (cosines - 1.0))

    def add_block(carried, resp, row_block):
        weighted = carried[0] + lax.dot_general(
            resp, row_block, (((0,), (0,)), ((), ())), preferred_element_type=jnp.float32
        )
        masses = carried[1] + jnp.sum(resp.astype(jnp.float32), axis=0)
        return (weighted, masses)

    local_centroids = centroids.shape[0]
    start_state = (
        jnp.zeros((local_centroids, centroids.shape[1]), jnp.float32),
        jnp.zeros((local_centroids,), jnp.float32),
    )
    partial_sums = lax.map(lambda row_block: jnp.sum(exponents(row_block), axis=1), grouped)
    totals = of_everyone(partial_sums, "blk")

    def accumulate(carried, element):
        row_block, block_totals = element
        resp = (exponents(row_block) / block_totals[:, None]).astype(jnp.bfloat16)
        return (add_block(carried, resp, row_block), None)

    (weighted, masses), _ = lax.scan(accumulate, start_state, (grouped, totals))
    factor = K / (row_total * lax.axis_size("rows"))
    share, share_masses = side_by_side((weighted, masses), "rows", 0, 1)
    new_share, weight_share = finish(share, share_masses, factor)
    return side_by_side_2((new_share, weight_share), "rows", 0, 1)


def solution(mesh):
    return jax.shard_map(
        local,
        mesh=mesh,
        in_specs=(P(("blk", "rows"), None), P("blk", None), P("blk")),
        out_specs=(P("blk", None), P("blk")),
        check_vma=False,
    )
```

profile of v0, /device:TPU:25, one launch (start us, length us, event | category | flops | bytes accessed | tf_op | source)
XLA Modules:
  0.0 280.6 jit_solution(1519887824641105736)
XLA Ops:
  7.2 1.5 fusion.11
  8.7 2.2 fusion.12
  11.0 0.4 fusion.9
  11.4 0.3 fusion.10
  11.7 88.0 %all-gather.3.cloned.1.call-done = bf16[4096,768]{1,0:T(8,128)(2,1)} async-done(((bf16[512,768]{1,0:T(8,128)(2,1)}), bf16[4096,768]{1,0:T(8,128)(2,1)}) %all-gather.3.cloned.1.call-update) | async-done | bytes 6291472 | tf_op jit(solution)/shard_map/all_gather | solution.py:77
  99.6 19.3 %while.27 = (s32[]{:T(128)}, f32[8,512]{1,0:T(8,128)S(1)}, f32[1024]{0:T(1024)S(1)}, bf16[8,512,768]{2,1,0:T(8,128)(2,1)}, bf16[1024,768]{1,0:T(8,128)(2,1)S(1)}, /*index=5*/s32[]{:T(128)}, s32[]{:T(128)}) while((s32[]{:T(128)}, f32[8,512]{1,0:T(8,128)S(1)}, f32[1024]{0:T(1024)S(1)}, bf16[8,512,768]{2,1,0:T(8,128)(2,1)}, ...), condition=%wide.region_4.5_spmd, body=%wide.region_2.4_spmd.sunk | while | flops 807403008 | bytes 2369629 | solution.py:100
  99.6 2.3 exponential_reduce_fusion.2
  102.0 0.1 dynamic_update_slice.8
  102.1 2.3 exponential_reduce_fusion.2
  104.4 0.1 dynamic_update_slice.8
  104.5 2.3 exponential_reduce_fusion.2
  106.8 0.1 dynamic_update_slice.8
  106.9 2.3 exponential_reduce_fusion.2
  109.2 0.1 dynamic_update_slice.8
  109.3 2.3 exponential_reduce_fusion.2
  111.7 2.3 exponential_reduce_fusion.2
  114.1 2.3 exponential_reduce_fusion.2
  116.5 2.3 exponential_reduce_fusion.2
  118.9 0.7 broadcast_in_dim.31
  119.6 5.1 %all-to-all-start = ((f32[8,8,512]{2,1,0:T(8,128)}), f32[8,8,512]{2,1,0:T(8,128)S(1)}, u32[]{:S(2)}, u32[]{:S(2)}) async-start(f32[8,8,512]{2,1,0:T(8,128)} %broadcast_in_dim.31), calls=%async_computation | async-start | bytes 262144 | tf_op jit(solution)/shard_map/all_to_all | solution.py:16
  124.8 4.8 %all-to-all-done = f32[8,8,512]{2,1,0:T(8,128)S(1)} async-done(((f32[8,8,512]{2,1,0:T(8,128)}), f32[8,8,512]{2,1,0:T(8,128)S(1)}, u32[]{:S(2)}, u32[]{:S(2)}) %all-to-all-start) | async-done | bytes 131104 | tf_op jit(solution)/shard_map/all_to_all | solution.py:16
  129.6 47.6 %while.28 = (s32[]{:T(128)}, f32[1024,768]{1,0:T(8,128)S(1)}, f32[1024]{0:T(1024)S(1)}, f32[1024]{0:T(1024)S(1)}, bf16[8,512,768]{2,1,0:T(8,128)(2,1)}, /*index=...) while((s32[]{:T(128)}, f32[1024,768]{1,0:T(8,128)S(1)}, ...), condition=%wide.region_8.9_spmd.clone, body=%wide.region_6.8_spmd.clone.sunk | while | flops 1615856640 | bytes 11561084 | solution.py:108
  129.7 2.9 %convert_reduce_fusion.2 = (f32[1024]{0:T(1024)S(1)}, bf16[512,1024]{1,0:T(8,128)(2,1)S(1)}) fusion(f32[512]{0:T(512)S(1)} %bitcast.36, bf16[1024,768]{1,0:T(8,128)(2,1)} %get-tuple-element.332, bf16[8,512,768]{2,1,0:T(8,128)(2,1)} %get-tuple-element.331, s32[]{:T(128)S(6)} %copy.17, f32[1024]{0:T(1024)S(1)} %get-tuple-element.330), kind=kOutput, calls=%fused_computation.5.clone.1 | convolution fusion | flops 808975360 | bytes 3418116 | tf_op jit(solution)/shard_map/while/body/eval_jaxpr/dot_general | solution.py:83
  132.6 3.0 %select_add_fusion.4 = f32[1024,768]{1,0:T(8,128)S(1)} fusion(f32[1024,768]{1,0:T(8,128)S(1)} %get-tuple-element.319, bf16[512,1024]{1,0:T(8,128)(2,1)S(1)} %get-tuple-element.286, pred[]{:T(512)S(6)} %compare.3, bf16[8,512,768]{2,1,0:T(8,128)(2,1)} %get-tuple-element.331, s32[]{:T(128)S(6)} %copy.17), kind=kOutput, calls=%fused_computation.4.clone.1 | convolution fusion | flops 806879232 | bytes 8126469 | tf_op jit(solution)/shard_map/while/body/eval_jaxpr/dot_general | solution.py:89
  135.6 2.9 %convert_reduce_fusion.2 = (f32[1024]{0:T(1024)S(1)}, bf16[512,1024]{1,0:T(8,128)(2,1)S(1)}) fusion(f32[512]{0:T(512)S(1)} %bitcast.36, bf16[1024,768]{1,0:T(8,128)(2,1)} %get-tuple-element.332, bf16[8,512,768]{2,1,0:T(8,128)(2,1)} %get-tuple-element.331, s32[]{:T(128)S(6)} %copy.17, f32[1024]{0:T(1024)S(1)} %get-tuple-element.330), kind=kOutput, calls=%fused_computation.5.clone.1 | convolution fusion | flops 808975360 | bytes 3418116 | tf_op jit(solution)/shard_map/while/body/eval_jaxpr/dot_general | solution.py:83
  138.5 3.0 %select_add_fusion.4 = f32[1024,768]{1,0:T(8,128)S(1)} fusion(f32[1024,768]{1,0:T(8,128)S(1)} %get-tuple-element.319, bf16[512,1024]{1,0:T(8,128)(2,1)S(1)} %get-tuple-element.286, pred[]{:T(512)S(6)} %compare.3, bf16[8,512,768]{2,1,0:T(8,128)(2,1)} %get-tuple-element.331, s32[]{:T(128)S(6)} %copy.17), kind=kOutput, calls=%fused_computation.4.clone.1 | convolution fusion | flops 806879232 | bytes 8126469 | tf_op jit(solution)/shard_map/while/body/eval_jaxpr/dot_general | solution.py:89
  141.6 2.9 %convert_reduce_fusion.2 = (f32[1024]{0:T(1024)S(1)}, bf16[512,1024]{1,0:T(8,128)(2,1)S(1)}) fusion(f32[512]{0:T(512)S(1)} %bitcast.36, bf16[1024,768]{1,0:T(8,128)(2,1)} %get-tuple-element.332, bf16[8,512,768]{2,1,0:T(8,128)(2,1)} %get-tuple-element.331, s32[]{:T(128)S(6)} %copy.17, f32[1024]{0:T(1024)S(1)} %get-tuple-element.330), kind=kOutput, calls=%fused_computation.5.clone.1 | convolution fusion | flops 808975360 | bytes 3418116 | tf_op jit(solution)/shard_map/while/body/eval_jaxpr/dot_general | solution.py:83
  144.5 3.0 %select_add_fusion.4 = f32[1024,768]{1,0:T(8,128)S(1)} fusion(f32[1024,768]{1,0:T(8,128)S(1)} %get-tuple-element.319, bf16[512,1024]{1,0:T(8,128)(2,1)S(1)} %get-tuple-element.286, pred[]{:T(512)S(6)} %compare.3, bf16[8,512,768]{2,1,0:T(8,128)(2,1)} %get-tuple-element.331, s32[]{:T(128)S(6)} %copy.17), kind=kOutput, calls=%fused_computation.4.clone.1 | convolution fusion | flops 806879232 | bytes 8126469 | tf_op jit(solution)/shard_map/while/body/eval_jaxpr/dot_general | solution.py:89
  147.5 2.9 %convert_reduce_fusion.2 = (f32[1024]{0:T(1024)S(1)}, bf16[512,1024]{1,0:T(8,128)(2,1)S(1)}) fusion(f32[512]{0:T(512)S(1)} %bitcast.36, bf16[1024,768]{1,0:T(8,128)(2,1)} %get-tuple-element.332, bf16[8,512,768]{2,1,0:T(8,128)(2,1)} %get-tuple-element.331, s32[]{:T(128)S(6)} %copy.17, f32[1024]{0:T(1024)S(1)} %get-tuple-element.330), kind=kOutput, calls=%fused_computation.5.clone.1 | convolution fusion | flops 808975360 | bytes 3418116 | tf_op jit(solution)/shard_map/while/body/eval_jaxpr/dot_general | solution.py:83
  150.4 3.0 %select_add_fusion.4 = f32[1024,768]{1,0:T(8,128)S(1)} fusion(f32[1024,768]{1,0:T(8,128)S(1)} %get-tuple-element.319, bf16[512,1024]{1,0:T(8,128)(2,1)S(1)} %get-tuple-element.286, pred[]{:T(512)S(6)} %compare.3, bf16[8,512,768]{2,1,0:T(8,128)(2,1)} %get-tuple-element.331, s32[]{:T(128)S(6)} %copy.17), kind=kOutput, calls=%fused_computation.4.clone.1 | convolution fusion | flops 806879232 | bytes 8126469 | tf_op jit(solution)/shard_map/while/body/eval_jaxpr/dot_general | solution.py:89
  153.5 2.9 %convert_reduce_fusion.2 = (f32[1024]{0:T(1024)S(1)}, bf16[512,1024]{1,0:T(8,128)(2,1)S(1)}) fusion(f32[512]{0:T(512)S(1)} %bitcast.36, bf16[1024,768]{1,0:T(8,128)(2,1)} %get-tuple-element.332, bf16[8,512,768]{2,1,0:T(8,128)(2,1)} %get-tuple-element.331, s32[]{:T(128)S(6)} %copy.17, f32[1024]{0:T(1024)S(1)} %get-tuple-element.330), kind=kOutput, calls=%fused_computation.5.clone.1 | convolution fusion | flops 808975360 | bytes 3418116 | tf_op jit(solution)/shard_map/while/body/eval_jaxpr/dot_general | solution.py:83
  156.4 3.0 %select_add_fusion.4 = f32[1024,768]{1,0:T(8,128)S(1)} fusion(f32[1024,768]{1,0:T(8,128)S(1)} %get-tuple-element.319, bf16[512,1024]{1,0:T(8,128)(2,1)S(1)} %get-tuple-element.286, pred[]{:T(512)S(6)} %compare.3, bf16[8,512,768]{2,1,0:T(8,128)(2,1)} %get-tuple-element.331, s32[]{:T(128)S(6)} %copy.17), kind=kOutput, calls=%fused_computation.4.clone.1 | convolution fusion | flops 806879232 | bytes 8126469 | tf_op jit(solution)/shard_map/while/body/eval_jaxpr/dot_general | solution.py:89
  159.4 2.9 %convert_reduce_fusion.2 = (f32[1024]{0:T(1024)S(1)}, bf16[512,1024]{1,0:T(8,128)(2,1)S(1)}) fusion(f32[512]{0:T(512)S(1)} %bitcast.36, bf16[1024,768]{1,0:T(8,128)(2,1)} %get-tuple-element.332, bf16[8,512,768]{2,1,0:T(8,128)(2,1)} %get-tuple-element.331, s32[]{:T(128)S(6)} %copy.17, f32[1024]{0:T(1024)S(1)} %get-tuple-element.330), kind=kOutput, calls=%fused_computation.5.clone.1 | convolution fusion | flops 808975360 | bytes 3418116 | tf_op jit(solution)/shard_map/while/body/eval_jaxpr/dot_general | solution.py:83
  162.3 3.0 %select_add_fusion.4 = f32[1024,768]{1,0:T(8,128)S(1)} fusion(f32[1024,768]{1,0:T(8,128)S(1)} %get-tuple-element.319, bf16[512,1024]{1,0:T(8,128)(2,1)S(1)} %get-tuple-element.286, pred[]{:T(512)S(6)} %compare.3, bf16[8,512,768]{2,1,0:T(8,128)(2,1)} %get-tuple-element.331, s32[]{:T(128)S(6)} %copy.17), kind=kOutput, calls=%fused_computation.4.clone.1 | convolution fusion | flops 806879232 | bytes 8126469 | tf_op jit(solution)/shard_map/while/body/eval_jaxpr/dot_general | solution.py:89
  165.4 2.9 %convert_reduce_fusion.2 = (f32[1024]{0:T(1024)S(1)}, bf16[512,1024]{1,0:T(8,128)(2,1)S(1)}) fusion(f32[512]{0:T(512)S(1)} %bitcast.36, bf16[1024,768]{1,0:T(8,128)(2,1)} %get-tuple-element.332, bf16[8,512,768]{2,1,0:T(8,128)(2,1)} %get-tuple-element.331, s32[]{:T(128)S(6)} %copy.17, f32[1024]{0:T(1024)S(1)} %get-tuple-element.330), kind=kOutput, calls=%fused_computation.5.clone.1 | convolution fusion | flops 808975360 | bytes 3418116 | tf_op jit(solution)/shard_map/while/body/eval_jaxpr/dot_general | solution.py:83
  168.3 3.0 %select_add_fusion.4 = f32[1024,768]{1,0:T(8,128)S(1)} fusion(f32[1024,768]{1,0:T(8,128)S(1)} %get-tuple-element.319, bf16[512,1024]{1,0:T(8,128)(2,1)S(1)} %get-tuple-element.286, pred[]{:T(512)S(6)} %compare.3, bf16[8,512,768]{2,1,0:T(8,128)(2,1)} %get-tuple-element.331, s32[]{:T(128)S(6)} %copy.17), kind=kOutput, calls=%fused_computation.4.clone.1 | convolution fusion | flops 806879232 | bytes 8126469 | tf_op jit(solution)/shard_map/while/body/eval_jaxpr/dot_general | solution.py:89
  171.3 2.9 %convert_reduce_fusion.2 = (f32[1024]{0:T(1024)S(1)}, bf16[512,1024]{1,0:T(8,128)(2,1)S(1)}) fusion(f32[512]{0:T(512)S(1)} %bitcast.36, bf16[1024,768]{1,0:T(8,128)(2,1)} %get-tuple-element.332, bf16[8,512,768]{2,1,0:T(8,128)(2,1)} %get-tuple-element.331, s32[]{:T(128)S(6)} %copy.17, f32[1024]{0:T(1024)S(1)} %get-tuple-element.330), kind=kOutput, calls=%fused_computation.5.clone.1 | convolution fusion | flops 808975360 | bytes 3418116 | tf_op jit(solution)/shard_map/while/body/eval_jaxpr/dot_general | solution.py:83
  174.3 3.0 %select_add_fusion.4 = f32[1024,768]{1,0:T(8,128)S(1)} fusion(f32[1024,768]{1,0:T(8,128)S(1)} %get-tuple-element.319, bf16[512,1024]{1,0:T(8,128)(2,1)S(1)} %get-tuple-element.286, pred[]{:T(512)S(6)} %compare.3, bf16[8,512,768]{2,1,0:T(8,128)(2,1)} %get-tuple-element.331, s32[]{:T(128)S(6)} %copy.17), kind=kOutput, calls=%fused_computation.4.clone.1 | convolution fusion | flops 806879232 | bytes 8126469 | tf_op jit(solution)/shard_map/while/body/eval_jaxpr/dot_general | solution.py:89
  177.3 1.1 concatenate.15
  178.4 1.4 pad_maximum_fusion
  179.8 50.9 %all_to_all.10 = f32[16,64,769]{2,1,0:T(8,128)} all-to-all(f32[16,64,769]{2,1,0:T(8,128)S(1)} %pad_maximum_fusion), channel_id=1, replica_groups=mesh['blk'=8,'rows'=16] {'rows'}, dimensions={0} | all-to-all | bytes 6299648 | tf_op jit(solution)/shard_map/all_to_all | solution.py:32
  230.7 2.2 reduce_sum.72
  232.9 0.1 multiply_reduce_fusion
  233.1 0.1 slice_multiply_fusion
  233.2 0.7 pad_maximum_fusion.1
  233.9 34.3 %all-gather.5.cloned.1.call-done = f32[1024,769]{1,0:T(8,128)} async-done(((f32[64,769]{1,0:T(8,128)}), f32[1024,769]{1,0:T(8,128)}) %all-gather.5.cloned.1.call-update) | async-done | bytes 3149840 | tf_op jit(solution)/shard_map/all_gather | solution.py:53
  268.2 1.8 slice_reduce_fusion
  270.0 3.8 %split.18 = f32[1024,768]{1,0:T(8,128)} slice(f32[1024,769]{1,0:T(8,128)} %all-gather.5.cloned.1.call-done), slice={[0:1024], [0:768]} | slice | bytes 6291456 | tf_op jit(solution)/shard_map/split | solution.py:54
  (38 shorter events, 0.5 us)
Async XLA Ops:
  7.2 3.8 %copy-start = (bf16[1024,768]{1,0:T(8,128)(2,1)S(1)}, bf16[1024,768]{1,0:T(8,128)(2,1)}, u32[]{:S(2)}) copy-start(bf16[1024,768]{1,0:T(8,128)(2,1)} %param.8) | copy-start | bytes 4718596
  7.2 92.5 %all-gather.3.cloned.1.call-start = ((), (), s32[]{:S(2)}) async-start(), calls=%async_computation.2 | async-start | bytes 7077888 | tf_op jit(solution)/shard_map/all_gather | solution.py:77
  11.0 88.7 %copy-start.2 = (f32[1024]{0:T(1024)S(1)}, f32[1024]{0:T(1024)}, u32[]{:S(2)}) copy-start(f32[1024]{0:T(1024)} %param.9) | copy-start | bytes 12292
  118.9 5.9 %copy-start.1 = (bf16[1024,768]{1,0:T(8,128)(2,1)}, bf16[1024,768]{1,0:T(8,128)(2,1)S(1)}, u32[]{:S(2)}) copy-start(bf16[1024,768]{1,0:T(8,128)(2,1)S(1)} %get-tuple-element.343) | copy-start | bytes 4718596
  119.6 10.0 %all-to-all-start = ((f32[8,8,512]{2,1,0:T(8,128)}), f32[8,8,512]{2,1,0:T(8,128)S(1)}, u32[]{:S(2)}, u32[]{:S(2)}) async-start(f32[8,8,512]{2,1,0:T(8,128)} %broadcast_in_dim.31), calls=%async_computation | async-start | bytes 262144 | tf_op jit(solution)/shard_map/all_to_all | solution.py:16
  124.8 143.4 %all-gather.5.cloned.1.call-start = ((), (), s32[]{:S(2)}) async-start(), calls=%async_computation.3 | async-start | bytes 3899392 | tf_op jit(solution)/shard_map/all_gather | solution.py:53
Sparse Core Ops, SparseCore 0:
  11.1 88.5 all-gather.2
  234.0 34.1 all-gather.4
where the time goes:
time: 283 us; the launch traced here: 281 us
  waiting for transfers between devices  127 us (45%)
  matrix products  65.8 us (23%)
  blocking collectives  50.9 us (18%)
  between operations  14.2 us (5%)
  other arithmetic  8.97 us (3%)
  local copies, waits for them, and re-layouts  7.99 us (3%)
  starting transfers between devices  5.18 us (2%)
    all_gather x1, waiting for transfers between devices, local(): gathered = lax.all_gather(row_units, 'blk', axis=0, tiled=True)  88 us
    all_to_all x1, blocking collectives, summed_on_arrival(): lax.all_to_all(pieces, axis, split_axis=0, concat_axis=0, tiled=True)  50.9 us
    dot_general x16, matrix products, exponents(): lax.dot_general(row_block, centroid_units, (((1,), (1,)), ((), ())), pref...  41.7 us
    all_gather x1, waiting for transfers between devices, side_by_side_2(): filled = lax.all_gather(both, axis, axis=dim, tiled=True)  34.3 us
    dot_general x8, matrix products, add_block(): lax.dot_general(resp, row_block, (((0,), (0,)), ((), ())), preferred_elem...  24 us
  transfers between devices with their start and end apart: 3, of which 3 were waited for; matrix products, arithmetic and copies ran while one was open for 0% of the time, Pallas kernels for 0%

commit v1 on v0

v1 whole, which is shorter than its diff:
```python
import math

import jax
import jax.numpy as jnp
from jax import lax
from jax.experimental import pallas as pl
from jax.experimental.pallas import tpu as pltpu
from jax.sharding import PartitionSpec as P

D = 768
CONCENTRATION = 32.0
LOG2E = 1.4426950408889634
MESH = pl.DeviceIdType.MESH
NT = (((1,), (1,)), ((), ()))
NN = (((1,), (0,)), ((), ()))

ROWS = 512
GROUPS = 4
PIECE = 64


def unit(v):
    v = v.astype(jnp.float32)
    return (v * lax.rsqrt(jnp.sum(v * v, axis=1, keepdims=True) + 1e-6)).astype(jnp.bfloat16)


def kernel(
    factor,
    emb, cen, lm, out, wout,
    xr, cr, xu, cu, lmh, lmc, sc, tr, ps, pb, ma, ra, rc, rs, fh, fr, ob, ms, mr, wo,
    in_sem, a_send, a_recv, d_send, d_recv, b_send, b_recv, t_send, t_recv,
    c_send, c_recv, r_send, r_recv, f_send, f_recv, m_send, m_recv, o_send, o_recv,
    q_send, q_recv, w_send, w_recv, out_sem,
):
    blk, row = lax.axis_index("blk"), lax.axis_index("rows")
    z, hi = blk // 2, blk % 2
    x, lo, c = row // 4, (row // 2) % 2, row % 2
    zp, zm, z2 = (z + 1) % 4, (z + 3) % 4, (z + 2) % 4
    xp, xm, x2 = (x + 1) % 4, (x + 3) % 4, (x + 2) % 4
    me8 = z * 2 + c

    def dev(z=z, hi=hi, x=x, lo=lo, c=c):
        return (z * 2 + hi, x * 4 + lo * 2 + c)

    def remote(src, dst, send, recv, to):
        return pltpu.make_async_remote_copy(
            src_ref=src, dst_ref=dst, send_sem=send, recv_sem=recv, device_id=to, device_id_type=MESH
        )

    started = []

    def go(src, dst, send, recv, to):
        copy = remote(src, dst, send, recv, to)
        copy.start()
        started.append(copy)

    def landed(dst, send, recv):
        remote(dst, dst, send, recv, dev(c=1 - c)).wait_recv()

    get_x = pltpu.make_async_copy(emb, xr, in_sem.at[0])
    get_c = pltpu.make_async_copy(cen.at[pl.ds(pl.multiple_of(c * 512, 512), 512)], cr, in_sem.at[1])
    get_x.start()
    get_c.start()

    line = [dev(c=1 - c)] + [dev(z=zz, c=cc) for zz in (zp, zm, z2) for cc in (0, 1)]
    near = [dev(lo=1 - lo)] + [dev(x=xx, lo=ll) for xx in (xp, xm, x2) for ll in (0, 1)]
    across = [dev(hi=1 - hi, x=xx, lo=ll) for xx in range(4) for ll in (0, 1)]
    barrier = pltpu.get_barrier_semaphore()
    for peer in line + near + across:
        pl.semaphore_signal(barrier, inc=1, device_id=peer, device_id_type=MESH)

    get_x.wait()

    def unit_rows(i, _):
        v = unit(xr[pl.ds(pl.multiple_of(i * 64, 64), 64)])
        xu[i // 2, z, c, pl.ds(pl.multiple_of(i % 2 * 64, 64), 64)] = v
        return 0

    lax.fori_loop(0, ROWS // 64, unit_rows, 0)
    get_c.wait()

    def unit_centroids(i, _):
        cu[i] = unit(cr[pl.ds(pl.multiple_of(i * 64, 64), 64)])
        return 0

    lax.fori_loop(0, 8, unit_centroids, 0)

    def offsets(i, ref, turn, base):
        r = ref[pl.ds(c * 4 + i, 1), :]
        wide = jnp.broadcast_to(r, (128, 128))
        if turn:
            wide = pltpu.roll(wide, 64, 1)
        lmc[base + i] = (wide.T - CONCENTRATION) * LOG2E

    for i in range(4):
        offsets(i, lm, False, 0)

    def clear(i, _):
        ps[i] = jnp.zeros((PIECE, D), jnp.float32)
        return 0

    lax.fori_loop(0, 16, clear, 0)
    ma[...] = jnp.zeros_like(ma)
    pl.semaphore_wait(barrier, len(line + near + across))

    def piece(g, zs, e):
        return xu.at[g, zs, c, pl.ds(e * 64, 64)]

    def rows_out(g):
        for e in (0, 1):
            at = piece(g, z, e)
            go(at, at, a_send.at[g, e], a_recv.at[g, e], dev(z=zp))
            go(at, at, a_send.at[g, 2 + e], a_recv.at[g, 2 + e], dev(z=zm))

    def share(g, zs, k):
        at = xu.at[g, zs, c]
        go(at, at, d_send.at[g, k], d_recv.at[g, k], dev(c=1 - c))

    def rows_came(g, zs, e, k):
        landed(piece(g, zs, e), a_send.at[g, k], a_recv.at[g, k])

    def neighbours_in(g):
        rows_came(g, zm, 0, 0)
        at = piece(g, zm, 0)
        go(at, at, a_send.at[g, 4], a_recv.at[g, 4], dev(z=zp))
        rows_came(g, zp, 1, 3)
        at = piece(g, zp, 1)
        go(at, at, a_send.at[g, 5], a_recv.at[g, 5], dev(z=zm))
        if g + 2 < GROUPS:
            rows_out(g + 2)
        rows_came(g, zm, 1, 1)
        share(g, zm, 1)
        rows_came(g, zp, 0, 2)
        share(g, zp, 2)

    def far_in(g):
        rows_came(g, z2, 0, 4)
        rows_came(g, z2, 1, 5)
        share(g, z2, 3)

    def shared(g):
        for zs, k in ((z, 0), (zm, 1), (zp, 2), (z2, 3)):
            landed(xu.at[g, zs, 1 - c], d_send.at[g, k], d_recv.at[g, k])

    rows_out(0)
    rows_out(1)
    for g in range(GROUPS):
        share(g, z, 0)
    opposite = dev(hi=1 - hi, lo=1 - lo)
    for i in range(8):
        copy = remote(cu.at[i], cu.at[8 + (i ^ 1)], b_send.at[0], b_recv.at[0], opposite)
        copy.start()
    go(lm, lmh, b_send.at[1], b_recv.at[1], opposite)

    def block(g, n):
        return xu[g, pl.ds(n * 2, 2)].reshape(512, D)

    def scores(g, h):
        def zero(n, _):
            tr[g, me8, n] = jnp.zeros((1, 512), jnp.float32)
            return 0

        def add(m, _):
            n, i = m // 2, m % 2
            cos = lax.dot_general(
                cu[pl.ds(h * 8 + i * 4, 4)].reshape(256, D), block(g, n), NT,
                preferred_element_type=jnp.float32,
            )
            off = lmc[pl.ds(h * 4 + i * 2, 2)].reshape(256, 128)
            off = jnp.concatenate([off] * 4, axis=1)
            e = jnp.exp2(cos * (CONCENTRATION * LOG2E) + off)
            sc[g, n, pl.ds(pl.multiple_of(h * 512 + i * 256, 256), 256)] = e
            tr[g, me8, n] = tr[g, me8, n] + jnp.sum(e, axis=0, keepdims=True)
            return 0

        if h == 0:
            lax.fori_loop(0, 2, zero, 0)
        lax.fori_loop(0, 4, add, 0)

    def totals_out(zs):
        for peer in line:
            remote(tr.at[zs, me8], tr.at[zs, me8], t_send.at[zs], t_recv.at[zs], peer).start()

    def totals_in(zs):
        all7 = tr.at[zs, pl.ds(0, 7)]
        landed(all7, t_send.at[zs], t_recv.at[zs])

    def inverse(zs):
        return 1.0 / jnp.sum(tr[zs], axis=0)

    def weigh(zs, begin, end):
        inv = inverse(zs)

        def body(i, _):
            acc = ps[pl.ds(i * 4, 4)].reshape(256, D)
            mass = ma[pl.ds(i * 2, 2)].reshape(256, 128)
            for plane in range(2):
                r = sc[zs, plane, pl.ds(pl.multiple_of(i * 256, 256), 256)] * inv[plane]
                for q in range(4):
                    mass = mass + r[:, q * 128 : (q + 1) * 128]
                acc = acc + lax.dot_general(
                    r.astype(jnp.bfloat16), block(zs, plane), NN, preferred_element_type=jnp.float32
                )
            ps[pl.ds(i * 4, 4)] = acc.reshape(4, PIECE, D)
            ma[pl.ds(i * 2, 2)] = mass.reshape(2, 128, 128)
            return 0

        lax.fori_loop(begin, end, body, 0)

    neighbours_in(0)
    neighbours_in(1)
    far_in(0)
    shared(0)
    scores(0, 0)
    neighbours_in(2)
    far_in(1)
    shared(1)
    scores(1, 0)
    landed(cu.at[pl.ds(8, 8)], b_send.at[0], b_recv.at[0])
    landed(lmh, b_send.at[1], b_recv.at[1])
    for i in range(4):
        offsets(i, lmh, True, 4)
    scores(0, 1)
    totals_out(0)
    scores(1, 1)
    totals_out(1)
    neighbours_in(3)
    far_in(2)
    totals_in(0)
    weigh(0, 0, 4)
    shared(2)
    scores(2, 0)
    scores(2, 1)
    totals_out(2)
    totals_in(1)
    weigh(1, 0, 4)
    far_in(3)
    shared(3)
    scores(3, 0)
    scores(3, 1)
    totals_out(3)
    totals_in(2)
    weigh(2, 0, 4)
    totals_in(3)

    def pack(ch):
        def body(i, _):
            pb[i] = ps[i].astype(jnp.bfloat16)
            return 0

        lax.fori_loop(ch * 8, ch * 8 + 8, body, 0)

    def scatter(ch):
        base = ch * 8

        def send(k, src, slot, to):
            go(src, rc.at[ch, slot], c_send.at[ch, k], c_recv.at[ch, slot], to)

        go(pb.at[base + x2 * 2], ra.at[ch, 0], r_send.at[ch, 0], r_recv.at[ch, 0], dev(x=xp))
        go(pb.at[base + x2 * 2 + 1], ra.at[ch, 1], r_send.at[ch, 1], r_recv.at[ch, 1], dev(x=xm))
        send(0, pb.at[base + xp * 2 + 1], lo, dev(x=xp, lo=1))
        send(1, pb.at[base + xm * 2], 2 + lo, dev(x=xm, lo=0))
        send(2, pb.at[base + x * 2 + 1 - lo], 4, dev(lo=1 - lo))

    def relay(ch):
        base = ch * 8
        landed(ra.at[ch, 0], r_send.at[ch, 0], r_recv.at[ch, 0])
        rs[ch, 0] = (ps[base + xp * 2] + ra[ch, 0].astype(jnp.float32)).astype(jnp.bfloat16)
        go(rs.at[ch, 0], rc.at[ch, lo], c_send.at[ch, 3], c_recv.at[ch, lo], dev(x=xp, lo=0))
        landed(ra.at[ch, 1], r_send.at[ch, 1], r_recv.at[ch, 1])
        rs[ch, 1] = (ps[base + xm * 2 + 1] + ra[ch, 1].astype(jnp.float32)).astype(jnp.bfloat16)
        go(rs.at[ch, 1], rc.at[ch, 2 + lo], c_send.at[ch, 4], c_recv.at[ch, 2 + lo], dev(x=xm, lo=1))

    def gathered(ch):
        total = ps[ch * 8 + x * 2 + lo]
        for slot in (4, 0, 1, 2, 3):
            landed(rc.at[ch, slot], c_send.at[ch, 0], c_recv.at[ch, slot])
            total = total + rc[ch, slot].astype(jnp.float32)
        return total

    weigh(3, 2, 4)
    pack(1)
    scatter(1)
    weigh(3, 0, 2)
    pack(0)
    scatter(0)

    for i in range(8):
        r = jnp.sum(ma[i].T, axis=0, keepdims=True)
        if i >= 4:
            r = pltpu.roll(jnp.broadcast_to(r, (8, 128)), 64, 1)[0:1]
        ms[i // 4, pl.ds(i % 4, 1)] = r
    mine = x * 2 + lo
    for peer in near:
        remote(ms.at[0], mr.at[mine], m_send, m_recv, peer).start()
    for peer in across:
        remote(ms.at[1], mr.at[8 + mine], m_send, m_recv, peer).start()
    mr[mine] = ms[0]

    relay(1)
    relay(0)
    fh[...] = gathered(1).astype(jnp.bfloat16)
    go(fh, fr, f_send.at[0], f_recv.at[0], opposite)
    total = gathered(0)
    landed(fr, f_send.at[0], f_recv.at[0])
    total = total + fr[...].astype(jnp.float32)
    done = total * lax.rsqrt(jnp.sum(total * total, axis=1, keepdims=True) + 1e-6)
    ob[c, x, lo] = done.astype(jnp.bfloat16)

    def hand(xx, ll, k, recv, to):
        at = ob.at[c, xx, ll]
        go(at, at, o_send.at[k], o_recv.at[recv], to)

    def handed(xx, ll, recv):
        landed(ob.at[c, xx, ll], o_send.at[0], o_recv.at[recv])

    def twin(xx, ll, k):
        at = ob.at[c, xx, ll]
        go(at, at, q_send.at[k], q_recv.at[k], dev(c=1 - c))

    for ll in (0, 1):
        hand(x, lo, ll, 1 + lo, dev(x=xp, lo=ll))
        hand(x, lo, 2 + ll, 3 + lo, dev(x=xm, lo=ll))
    hand(x, lo, 4, 0, dev(lo=1 - lo))
    twin(x, lo, 0)

    landed(mr.at[pl.ds(0, 15)], m_send, m_recv)
    wo[c] = jnp.sum(mr[...], axis=0) * factor
    go(wo.at[c], wo.at[c], w_send.at[0], w_recv.at[0], dev(c=1 - c))

    handed(xm, 0, 1)
    hand(xm, 0, 5, 5, dev(x=xp))
    handed(xp, 1, 4)
    hand(xp, 1, 6, 6, dev(x=xm))
    twin(xm, 0, 1)
    twin(xp, 1, 2)
    handed(xm, 1, 2)
    twin(xm, 1, 3)
    handed(xp, 0, 3)
    twin(xp, 0, 4)
    handed(x, 1 - lo, 0)
    twin(x, 1 - lo, 5)
    handed(x2, 0, 5)
    twin(x2, 0, 6)
    handed(x2, 1, 6)
    twin(x2, 1, 7)
    for k, (xx, ll) in enumerate(
        ((x, lo), (xm, 0), (xp, 1), (xm, 1), (xp, 0), (x, 1 - lo), (x2, 0), (x2, 1))
    ):
        landed(ob.at[1 - c, xx, ll], q_send.at[k], q_recv.at[k])
    landed(wo.at[1 - c], w_send.at[0], w_recv.at[0])
    put = pltpu.make_async_copy(ob, out, out_sem.at[0])
    put.start()
    put_w = pltpu.make_async_copy(wo, wout, out_sem.at[1])
    put_w.start()

    for copy in started:
        copy.wait_send()
    everything = dev(c=1 - c)
    remote(cu.at[pl.ds(8, 8)], cu.at[pl.ds(8, 8)], b_send.at[0], b_recv.at[0], everything).wait_send()
    for zs in range(4):
        all7 = tr.at[zs, pl.ds(0, 7)]
        remote(all7, all7, t_send.at[zs], t_recv.at[zs], everything).wait_send()
    m15 = mr.at[pl.ds(0, 15)]
    remote(m15, m15, m_send, m_recv, everything).wait_send()
    put.wait()
    put_w.wait()


def local(embeddings, centroids, log_mix, factor):
    f32, bf16 = jnp.float32, jnp.bfloat16
    dma = pltpu.SemaphoreType.DMA
    vmem = pltpu.VMEM
    any_spec = pl.BlockSpec(memory_space=pl.ANY)
    body = lambda *refs: kernel(factor, *refs)
    made, weights = pl.pallas_call(
        body,
        out_shape=(
            jax.ShapeDtypeStruct((2, 4, 2, PIECE, D), bf16),
            jax.ShapeDtypeStruct((2, 4, 128), f32),
        ),
        in_specs=[any_spec, any_spec, pl.BlockSpec(memory_space=vmem)],
        out_specs=(any_spec, any_spec),
        scratch_shapes=[
            vmem((ROWS, D), bf16),
            vmem((512, D), bf16),
            vmem((GROUPS, 4, 2, 128, D), bf16),
            vmem((16, PIECE, D), bf16),
            vmem((8, 128), f32),
            vmem((8, 128, 128), f32),
            vmem((4, 2, 1024, ROWS), f32),
            vmem((4, 8, 2, 1, ROWS), f32),
            vmem((16, PIECE, D), f32),
            vmem((16, PIECE, D), bf16),
            vmem((8, 128, 128), f32),
            vmem((2, 2, PIECE, D), bf16),
            vmem((2, 5, PIECE, D), bf16),
            vmem((2, 2, PIECE, D), bf16),
            vmem((PIECE, D), bf16),
            vmem((PIECE, D), bf16),
            vmem((2, 4, 2, PIECE, D), bf16),
            vmem((2, 4, 128), f32),
            vmem((16, 4, 128), f32),
            vmem((2, 4, 128), f32),
            dma((2,)),
            dma((GROUPS, 6)), dma((GROUPS, 6)),
            dma((GROUPS, 4)), dma((GROUPS, 4)),
            dma((2,)), dma((2,)),
            dma((4,)), dma((4,)),
            dma((2, 5)), dma((2, 5)),
            dma((2, 2)), dma((2, 2)),
            dma((1,)), dma((1,)),
            dma, dma,
            dma((7,)), dma((7,)),
            dma((8,)), dma((8,)),
            dma((1,)), dma((1,)),
            dma((2,)),
        ],
        compiler_params=pltpu.CompilerParams(
            collective_id=0, has_side_effects=True, vmem_limit_bytes=60 * 1024 * 1024
        ),
        cost_estimate=pl.CostEstimate(flops=13 * 10**9, bytes_accessed=10**7, transcendentals=4 * 10**6),
        name="em_step",
    )(embeddings, centroids, log_mix.reshape(8, 128))
    return made.reshape(1024, D).astype(f32), weights.reshape(1024)


def solution(mesh):
    blks, rows = mesh.shape["blk"], mesh.shape["rows"]

    def step(embeddings, centroids, log_mix):
        factor = centroids.shape[0] * blks / (embeddings.shape[0] * blks * rows)
        return local(embeddings, centroids, log_mix, factor)

    return jax.shard_map(
        step,
        mesh=mesh,
        in_specs=(P(("blk", "rows"), None), P("blk", None), P("blk")),
        out_specs=(P("blk", None), P("blk")),
        check_vma=False,
    )
```

time: 283 us -> 91.2 us (0.32)
  waiting for transfers between devices: 127 us -> 0 us
  Pallas kernels: 0 us -> 85.4 us
  matrix products: 65.8 us -> 0 us
  blocking collectives: 50.9 us -> 0 us
  between operations: 14.2 us -> 0.65 us
  local copies, waits for them, and re-layouts: 7.99 us -> 0.6 us
  other arithmetic: 8.97 us -> 3.31 us
  starting transfers between devices: 5.18 us -> 0 us
    all_gather x2 -> x0, waiting for transfers between devices: 122 us -> none  [the longest x1 88 us: local(): gathered = lax.all_gather(row_units, 'blk', axis=0, tiled=True)]
    pallas_call x0 -> x1, Pallas kernels: none -> 85.4 us  [local(): pl.pallas_call(body, out_shape=(jax.ShapeDtypeStruct((2, 4, 2, PIECE, D),...]
    dot_general x24 -> x0, matrix products: 65.8 us -> none  [the longest x16 41.7 us: exponents(): lax.dot_general(row_block, centroid_units, (((1,), (1,)), ((), ())), pref...]
    all_to_all x1 -> x0, blocking collectives: 50.9 us -> none  [summed_on_arrival(): lax.all_to_all(pieces, axis, split_axis=0, concat_axis=0, tiled=True)]
    split x2 -> x0, local copies, waits for them, and re-layouts: 5.6 us -> none  [side_by_side_2(): jnp.split(filled, [sum(widths[:k]) for k in range(1, len(widths))], axis=...]
    all_to_all x1 -> x0, starting transfers between devices: 5.14 us -> none  [sent_to_all(): lax.all_to_all(jnp.broadcast_to(x[None], (count, *x.shape)), axis, 0, 0,...]
    all_to_all x1 -> x0, waiting for transfers between devices: 4.82 us -> none  [sent_to_all(): lax.all_to_all(jnp.broadcast_to(x[None], (count, *x.shape)), axis, 0, 0,...]
    reduce_sum x5 -> x0, other arithmetic: 4.21 us -> none  [the longest x1 2.24 us: summed_on_arrival(): return arrived.sum(axis=0)]
  transfers between devices with their start and end apart: 3 -> 0, of which waited for: 3 -> 0; matrix products, arithmetic and copies ran while one was open for 0% -> 0% of each run, Pallas kernels for 0% -> 0%
where the time goes in v1:
time: 91.2 us; the launch traced here: 90 us
  Pallas kernels  85.4 us (94%)
  other arithmetic  3.31 us (4%)
    pallas_call x1, Pallas kernels, local(): pl.pallas_call(body, out_shape=(jax.ShapeDtypeStruct((2, 4, 2, PIECE, D),...  85.4 us
    convert_element_type x1, other arithmetic, local(): return (made.reshape(1024, D).astype(f32), weights.reshape(1024))  3.31 us

profile of v1, /device:TPU:25, one launch (start us, length us, event | category | flops | bytes accessed | tf_op | source)
XLA Modules:
  0.0 90.0 jit_solution(5519161265102985167)
XLA Ops:
  0.6 85.4 %em_step.1 = (bf16[2,4,2,64,768]{4,3,2,1,0:T(8,128)(2,1)}, f32[2,4,128]{2,1,0:T(4,128)}) custom-call(bf16[512,768]{1,0:T(8,128)(2,1)} %refs_0_.1, bf16[1024,768]{1,0:T(8,128)(2,1)} %refs_1_.1, f32[8,128]{1,0:T(8,128)} %bitcast.6), custom_call_target="tpu_custom_call" | custom-call | flops 12999999488 | bytes 10000000 | tf_op jit(solution)/shard_map/em_step/pallas_call | solution.py:376
  86.0 0.0 copy-start
  86.0 3.3 %bitcast_convert_fusion = f32[1024,768]{1,0:T(8,128)} fusion(bf16[2,4,2,64,768]{4,3,2,1,0:T(8,128)(2,1)} %get-tuple-element.4), kind=kLoop, calls=%fused_computation | loop fusion | flops 786432 | bytes 4718592 | tf_op jit(solution)/shard_map/convert_element_type | solution.py:425
  89.4 0.0 copy-done
  89.4 0.6 copy.6
Async XLA Ops:
  86.0 3.3 %copy-start = (f32[2,4,128]{2,1,0:T(4,128)S(1)}, f32[2,4,128]{2,1,0:T(4,128)}, u32[]{:S(2)}) copy-start(f32[2,4,128]{2,1,0:T(4,128)} %get-tuple-element.5) | copy-start | bytes 12292

commit v2 on v1

--- a/solution.py
+++ b/solution.py
@@ -152,30 +152,20 @@
         copy.start()
     go(lm, lmh, b_send.at[1], b_recv.at[1], opposite)
 
-    def block(g, n):
-        return xu[g, pl.ds(n * 2, 2)].reshape(512, D)
-
     def scores(g, h):
-        def zero(n, _):
-            tr[g, me8, n] = jnp.zeros((1, 512), jnp.float32)
-            return 0
-
-        def add(m, _):
-            n, i = m // 2, m % 2
+        def add(n, _):
             cos = lax.dot_general(
-                cu[pl.ds(h * 8 + i * 4, 4)].reshape(256, D), block(g, n), NT,
+                cu[pl.ds(h * 8, 8)].reshape(512, D), xu[g, n].reshape(256, D), NT,
                 preferred_element_type=jnp.float32,
             )
-            off = lmc[pl.ds(h * 4 + i * 2, 2)].reshape(256, 128)
-            off = jnp.concatenate([off] * 4, axis=1)
-            e = jnp.exp2(cos * (CONCENTRATION * LOG2E) + off)
-            sc[g, n, pl.ds(pl.multiple_of(h * 512 + i * 256, 256), 256)] = e
-            tr[g, me8, n] = tr[g, me8, n] + jnp.sum(e, axis=0, keepdims=True)
+            off = lmc[pl.ds(h * 4, 4)].reshape(512, 128)
+            e = jnp.exp2(cos * (CONCENTRATION * LOG2E) + jnp.concatenate([off] * 2, axis=1))
+            sc[g, n, pl.ds(h * 512, 512)] = e
+            part = jnp.sum(e, axis=0, keepdims=True)
+            tr[g, me8, n] = part if h == 0 else tr[g, me8, n] + part
             return 0
 
-        if h == 0:
-            lax.fori_loop(0, 2, zero, 0)
-        lax.fori_loop(0, 4, add, 0)
+        lax.fori_loop(0, 4, add, 0, unroll=4)
 
     def totals_out(zs):
         for peer in line:
@@ -188,24 +178,25 @@
     def inverse(zs):
         return 1.0 / jnp.sum(tr[zs], axis=0)
 
-    def weigh(zs, begin, end):
-        inv = inverse(zs)
+    def weigh(g, begin, end):
+        inv = inverse(g)
 
         def body(i, _):
             acc = ps[pl.ds(i * 4, 4)].reshape(256, D)
             mass = ma[pl.ds(i * 2, 2)].reshape(256, 128)
-            for plane in range(2):
-                r = sc[zs, plane, pl.ds(pl.multiple_of(i * 256, 256), 256)] * inv[plane]
-                for q in range(4):
-                    mass = mass + r[:, q * 128 : (q + 1) * 128]
-                acc = acc + lax.dot_general(
-                    r.astype(jnp.bfloat16), block(zs, plane), NN, preferred_element_type=jnp.float32
-                )
+            resp = []
+            for n in range(4):
+                r = sc[g, n, pl.ds(pl.multiple_of(i * 256, 256), 256)] * inv[n]
+                mass = mass + r[:, :128] + r[:, 128:]
+                resp.append(r.astype(jnp.bfloat16))
+            acc = acc + lax.dot_general(
+                jnp.concatenate(resp, axis=1), xu[g].reshape(1024, D), NN, preferred_element_type=jnp.float32
+            )
             ps[pl.ds(i * 4, 4)] = acc.reshape(4, PIECE, D)
             ma[pl.ds(i * 2, 2)] = mass.reshape(2, 128, 128)
             return 0
 
-        lax.fori_loop(begin, end, body, 0)
+        lax.fori_loop(begin, end, body, 0, unroll=2)
 
     neighbours_in(0)
     neighbours_in(1)
@@ -299,11 +290,11 @@
 
     relay(1)
     relay(0)
-    fh[...] = gathered(1).astype(jnp.bfloat16)
+    fh[...] = gathered(1)
     go(fh, fr, f_send.at[0], f_recv.at[0], opposite)
     total = gathered(0)
     landed(fr, f_send.at[0], f_recv.at[0])
-    total = total + fr[...].astype(jnp.float32)
+    total = total + fr[...]
     done = total * lax.rsqrt(jnp.sum(total * total, axis=1, keepdims=True) + 1e-6)
     ob[c, x, lo] = done.astype(jnp.bfloat16)
 
@@ -388,16 +379,16 @@
             vmem((16, PIECE, D), bf16),
             vmem((8, 128), f32),
             vmem((8, 128, 128), f32),
-            vmem((4, 2, 1024, ROWS), f32),
-            vmem((4, 8, 2, 1, ROWS), f32),
+            vmem((4, 4, 1024, 256), f32),
+            vmem((4, 8, 4, 1, 256), f32),
             vmem((16, PIECE, D), f32),
             vmem((16, PIECE, D), bf16),
             vmem((8, 128, 128), f32),
             vmem((2, 2, PIECE, D), bf16),
             vmem((2, 5, PIECE, D), bf16),
             vmem((2, 2, PIECE, D), bf16),
-            vmem((PIECE, D), bf16),
-            vmem((PIECE, D), bf16),
+            vmem((PIECE, D), f32),
+            vmem((PIECE, D), f32),
             vmem((2, 4, 2, PIECE, D), bf16),
             vmem((2, 4, 128), f32),
             vmem((16, 4, 128), f32),

time: 91.2 us -> 87.4 us (0.958)
  Pallas kernels: 85.4 us -> 81.4 us
    pallas_call x1, Pallas kernels: 85.4 us -> 81.4 us  [local(): pl.pallas_call(body, out_shape=(jax.ShapeDtypeStruct((2, 4, 2, PIECE, D),...]
where the time goes in v2:
time: 87.4 us; the launch traced here: 86 us
  Pallas kernels  81.4 us (93%)
  other arithmetic  3.31 us (4%)
    pallas_call x1, Pallas kernels, local(): pl.pallas_call(body, out_shape=(jax.ShapeDtypeStruct((2, 4, 2, PIECE, D),...  81.4 us
    convert_element_type x1, other arithmetic, local(): return (made.reshape(1024, D).astype(f32), weights.reshape(1024))  3.31 us

profile of v2, /device:TPU:25, one launch (start us, length us, event | category | flops | bytes accessed | tf_op | source)
XLA Modules:
  0.0 86.0 jit_solution(12441741572938810221)
XLA Ops:
  0.6 81.4 %em_step.1 = (bf16[2,4,2,64,768]{4,3,2,1,0:T(8,128)(2,1)}, f32[2,4,128]{2,1,0:T(4,128)}) custom-call(bf16[512,768]{1,0:T(8,128)(2,1)} %refs_0_.1, bf16[1024,768]{1,0:T(8,128)(2,1)} %refs_1_.1, f32[8,128]{1,0:T(8,128)} %bitcast.6), custom_call_target="tpu_custom_call" | custom-call | flops 12999999488 | bytes 10000000 | tf_op jit(solution)/shard_map/em_step/pallas_call | solution.py:367
  82.1 0.0 copy-start
  82.1 3.3 %bitcast_convert_fusion = f32[1024,768]{1,0:T(8,128)} fusion(bf16[2,4,2,64,768]{4,3,2,1,0:T(8,128)(2,1)} %get-tuple-element.4), kind=kLoop, calls=%fused_computation | loop fusion | flops 786432 | bytes 4718592 | tf_op jit(solution)/shard_map/convert_element_type | solution.py:416
  85.4 0.0 copy-done
  85.4 0.6 copy.6
Async XLA Ops:
  82.1 3.3 %copy-start = (f32[2,4,128]{2,1,0:T(4,128)S(1)}, f32[2,4,128]{2,1,0:T(4,128)}, u32[]{:S(2)}) copy-start(f32[2,4,128]{2,1,0:T(4,128)} %get-tuple-element.5) | copy-start | bytes 12292

commit v3 on v2

--- a/solution.py
+++ b/solution.py
@@ -37,7 +37,6 @@
     x, lo, c = row // 4, (row // 2) % 2, row % 2
     zp, zm, z2 = (z + 1) % 4, (z + 3) % 4, (z + 2) % 4
     xp, xm, x2 = (x + 1) % 4, (x + 3) % 4, (x + 2) % 4
-    me8 = z * 2 + c
 
     def dev(z=z, hi=hi, x=x, lo=lo, c=c):
         return (z * 2 + hi, x * 4 + lo * 2 + c)
@@ -62,9 +61,15 @@
     get_x.start()
     get_c.start()
 
-    line = [dev(c=1 - c)] + [dev(z=zz, c=cc) for zz in (zp, zm, z2) for cc in (0, 1)]
+    twin_core = dev(c=1 - c)
+    beside = [dev(hi=1 - hi, lo=1 - lo, c=cc) for cc in (0, 1)]
+
+    def end_of(zz):
+        return [dev(z=zz, c=cc) for cc in (0, 1)] + [dev(z=zz, hi=1 - hi, lo=1 - lo, c=cc) for cc in (0, 1)]
+
+    line = [twin_core] + beside + end_of(zp) + end_of(zm)
     near = [dev(lo=1 - lo)] + [dev(x=xx, lo=ll) for xx in (xp, xm, x2) for ll in (0, 1)]
-    across = [dev(hi=1 - hi, x=xx, lo=ll) for xx in range(4) for ll in (0, 1)]
+    across = [dev(z=z2, x=xx, lo=ll) for xx in range(4) for ll in (0, 1)]
     barrier = pltpu.get_barrier_semaphore()
     for peer in line + near + across:
         pl.semaphore_signal(barrier, inc=1, device_id=peer, device_id_type=MESH)
@@ -73,7 +78,8 @@
 
     def unit_rows(i, _):
         v = unit(xr[pl.ds(pl.multiple_of(i * 64, 64), 64)])
-        xu[i // 2, z, c, pl.ds(pl.multiple_of(i % 2 * 64, 64), 64)] = v
+        e = i % 2
+        xu[i // 2, ((z + e) % 2) * 2 + e, hi, c] = v
         return 0
 
     lax.fori_loop(0, ROWS // 64, unit_rows, 0)
@@ -85,15 +91,13 @@
 
     lax.fori_loop(0, 8, unit_centroids, 0)
 
-    def offsets(i, ref, turn, base):
+    def offsets(i, ref, base):
         r = ref[pl.ds(c * 4 + i, 1), :]
         wide = jnp.broadcast_to(r, (128, 128))
-        if turn:
-            wide = pltpu.roll(wide, 64, 1)
         lmc[base + i] = (wide.T - CONCENTRATION) * LOG2E
 
     for i in range(4):
-        offsets(i, lm, False, 0)
+        offsets(i, lm, 0)
 
     def clear(i, _):
         ps[i] = jnp.zeros((PIECE, D), jnp.float32)
@@ -103,54 +107,94 @@
     ma[...] = jnp.zeros_like(ma)
     pl.semaphore_wait(barrier, len(line + near + across))
 
-    def piece(g, zs, e):
-        return xu.at[g, zs, c, pl.ds(e * 64, 64)]
-
-    def rows_out(g):
-        for e in (0, 1):
-            at = piece(g, z, e)
-            go(at, at, a_send.at[g, e], a_recv.at[g, e], dev(z=zp))
-            go(at, at, a_send.at[g, 2 + e], a_recv.at[g, 2 + e], dev(z=zm))
-
-    def share(g, zs, k):
-        at = xu.at[g, zs, c]
-        go(at, at, d_send.at[g, k], d_recv.at[g, k], dev(c=1 - c))
-
-    def rows_came(g, zs, e, k):
-        landed(piece(g, zs, e), a_send.at[g, k], a_recv.at[g, k])
-
-    def neighbours_in(g):
-        rows_came(g, zm, 0, 0)
-        at = piece(g, zm, 0)
-        go(at, at, a_send.at[g, 4], a_recv.at[g, 4], dev(z=zp))
-        rows_came(g, zp, 1, 3)
-        at = piece(g, zp, 1)
-        go(at, at, a_send.at[g, 5], a_recv.at[g, 5], dev(z=zm))
-        if g + 2 < GROUPS:
-            rows_out(g + 2)
-        rows_came(g, zm, 1, 1)
-        share(g, zm, 1)
-        rows_came(g, zp, 0, 2)
-        share(g, zp, 2)
-
-    def far_in(g):
-        rows_came(g, z2, 0, 4)
-        rows_came(g, z2, 1, 5)
-        share(g, z2, 3)
+    up, down = (z % 2) * 2, ((z + 1) % 2) * 2 + 1
+    from_up, from_down = (z % 2) * 2 + 1, ((z + 1) % 2) * 2
+    opposite = dev(hi=1 - hi, lo=1 - lo)
+
+    def send_rows(g, slot, h, k, to):
+        at = xu.at[g, slot, h, c]
+        go(at, at, a_send.at[g, k], a_recv.at[g, k], to)
+
+    def rows_came(g, slot, h, k):
+        landed(xu.at[g, slot, h, c], a_send.at[g, k], a_recv.at[g, k])
+
+    def across_out(g):
+        send_rows(g, up, hi, 0, opposite)
+        send_rows(g, down, hi, 1, opposite)
+
+    def along_out(g):
+        send_rows(g, up, hi, 2, dev(z=zp))
+        send_rows(g, down, hi, 3, dev(z=zm))
+
+    def share(g, slot, h, k):
+        at = xu.at[g, slot, h, c]
+        go(at, at, d_send.at[g, k], d_recv.at[g, k], twin_core)
+
+    def relay_rows(g):
+        rows_came(g, up, 1 - hi, 0)
+        send_rows(g, up, 1 - hi, 4, dev(z=zp))
+        rows_came(g, down, 1 - hi, 1)
+        send_rows(g, down, 1 - hi, 5, dev(z=zm))
+        share(g, up, 1 - hi, 2)
+        share(g, down, 1 - hi, 3)
+
+    def near_rows(g):
+        rows_came(g, from_down, hi, 2)
+        share(g, from_down, hi, 4)
+        rows_came(g, from_up, hi, 3)
+        share(g, from_up, hi, 5)
+
+    def far_rows(g):
+        rows_came(g, from_down, 1 - hi, 4)
+        share(g, from_down, 1 - hi, 6)
+        rows_came(g, from_up, 1 - hi, 5)
+        share(g, from_up, 1 - hi, 7)
 
     def shared(g):
-        for zs, k in ((z, 0), (zm, 1), (zp, 2), (z2, 3)):
-            landed(xu.at[g, zs, 1 - c], d_send.at[g, k], d_recv.at[g, k])
-
-    rows_out(0)
-    rows_out(1)
+        for k, (slot, h) in enumerate((
+            (up, hi), (down, hi), (up, 1 - hi), (down, 1 - hi),
+            (from_down, hi), (from_up, hi), (from_down, 1 - hi), (from_up, 1 - hi),
+        )):
+            landed(xu.at[g, slot, h, 1 - c], d_send.at[g, k], d_recv.at[g, k])
+
+    def slice_to(xx, ll, k, recv, to):
+        at = cu.at[8 + xx * 2 + ll]
+        go(at, at, b_send.at[k], b_recv.at[recv], to)
+
+    def slice_came(xx, ll, recv):
+        landed(cu.at[8 + xx * 2 + ll], b_send.at[0], b_recv.at[recv])
+
+    across_out(0)
+    here = x * 2 + lo
+    go(cu.at[here], cu.at[8 + here], b_send.at[7], b_recv.at[7], dev(z=z2))
+    go(lm, lmh, b_send.at[8], b_recv.at[8], dev(z=z2))
+    along_out(0)
+    for g in range(1, GROUPS):
+        across_out(g)
+    along_out(1)
     for g in range(GROUPS):
-        share(g, z, 0)
-    opposite = dev(hi=1 - hi, lo=1 - lo)
-    for i in range(8):
-        copy = remote(cu.at[i], cu.at[8 + (i ^ 1)], b_send.at[0], b_recv.at[0], opposite)
-        copy.start()
-    go(lm, lmh, b_send.at[1], b_recv.at[1], opposite)
+        share(g, up, hi, 0)
+        share(g, down, hi, 1)
+
+    def slices_out():
+        slice_came(x, lo, 7)
+        slice_to(x, lo, 4, 0, dev(lo=1 - lo))
+        for ll in (0, 1):
+            slice_to(x, lo, ll, 1 + lo, dev(x=xp, lo=ll))
+            slice_to(x, lo, 2 + ll, 3 + lo, dev(x=xm, lo=ll))
+
+    def slices_on():
+        slice_came(xm, 0, 1)
+        slice_to(xm, 0, 5, 5, dev(x=xp))
+        slice_came(xp, 1, 4)
+        slice_to(xp, 1, 6, 6, dev(x=xm))
+
+    def slices_in():
+        slice_came(xm, 1, 2)
+        slice_came(xp, 0, 3)
+        slice_came(x, 1 - lo, 0)
+        slice_came(x2, 0, 5)
+        slice_came(x2, 1, 6)
 
     def scores(g, h):
         def add(n, _):
@@ -162,21 +206,25 @@
             e = jnp.exp2(cos * (CONCENTRATION * LOG2E) + jnp.concatenate([off] * 2, axis=1))
             sc[g, n, pl.ds(h * 512, 512)] = e
             part = jnp.sum(e, axis=0, keepdims=True)
-            tr[g, me8, n] = part if h == 0 else tr[g, me8, n] + part
+            side = n // 2
+            me = ((z + side) % 2) * 4 + hi * 2 + c
+            tr[g, side, me, n % 2] = part if h == 0 else tr[g, side, me, n % 2] + part
             return 0
 
         lax.fori_loop(0, 4, add, 0, unroll=4)
 
-    def totals_out(zs):
-        for peer in line:
-            remote(tr.at[zs, me8], tr.at[zs, me8], t_send.at[zs], t_recv.at[zs], peer).start()
-
-    def totals_in(zs):
-        all7 = tr.at[zs, pl.ds(0, 7)]
-        landed(all7, t_send.at[zs], t_recv.at[zs])
-
-    def inverse(zs):
-        return 1.0 / jnp.sum(tr[zs], axis=0)
+    def totals_out(g):
+        for side, me, ends in ((z % 2, hi * 2 + c, end_of(zp)), ((z + 1) % 2, 4 + hi * 2 + c, end_of(zm))):
+            at = tr.at[g, side, me]
+            for peer in [twin_core] + beside + ends:
+                remote(at, at, t_send.at[g, side], t_recv.at[g, side], peer).start()
+
+    def totals_in(g):
+        for side in (0, 1):
+            landed(tr.at[g, side, pl.ds(0, 7)], t_send.at[g, side], t_recv.at[g, side])
+
+    def inverse(g):
+        return 1.0 / jnp.sum(tr[g], axis=1)
 
     def weigh(g, begin, end):
         inv = inverse(g)
@@ -186,7 +234,7 @@
             mass = ma[pl.ds(i * 2, 2)].reshape(256, 128)
             resp = []
             for n in range(4):
-                r = sc[g, n, pl.ds(pl.multiple_of(i * 256, 256), 256)] * inv[n]
+                r = sc[g, n, pl.ds(pl.multiple_of(i * 256, 256), 256)] * inv[n // 2, n % 2]
                 mass = mass + r[:, :128] + r[:, 128:]
                 resp.append(r.astype(jnp.bfloat16))
             acc = acc + lax.dot_general(
@@ -198,38 +246,46 @@
 
         lax.fori_loop(begin, end, body, 0, unroll=2)
 
-    neighbours_in(0)
-    neighbours_in(1)
-    far_in(0)
+    relay_rows(0)
+    along_out(2)
+    slices_out()
+    near_rows(0)
+    relay_rows(1)
+    along_out(3)
+    slices_on()
+    far_rows(0)
+    relay_rows(2)
+    near_rows(1)
     shared(0)
     scores(0, 0)
-    neighbours_in(2)
-    far_in(1)
+    far_rows(1)
+    relay_rows(3)
+    slices_in()
+    near_rows(2)
+    landed(lmh, b_send.at[8], b_recv.at[8])
+    for i in range(4):
+        offsets(i, lmh, 4)
+    scores(0, 1)
+    totals_out(0)
     shared(1)
     scores(1, 0)
-    landed(cu.at[pl.ds(8, 8)], b_send.at[0], b_recv.at[0])
-    landed(lmh, b_send.at[1], b_recv.at[1])
-    for i in range(4):
-        offsets(i, lmh, True, 4)
-    scores(0, 1)
-    totals_out(0)
     scores(1, 1)
     totals_out(1)
-    neighbours_in(3)
-    far_in(2)
+    far_rows(2)
+    near_rows(3)
     totals_in(0)
     weigh(0, 0, 4)
+    far_rows(3)
     shared(2)
     scores(2, 0)
     scores(2, 1)
     totals_out(2)
-    totals_in(1)
-    weigh(1, 0, 4)
-    far_in(3)
     shared(3)
     scores(3, 0)
     scores(3, 1)
     totals_out(3)
+    totals_in(1)
+    weigh(1, 0, 4)
     totals_in(2)
     weigh(2, 0, 4)
     totals_in(3)
@@ -278,8 +334,6 @@
 
     for i in range(8):
         r = jnp.sum(ma[i].T, axis=0, keepdims=True)
-        if i >= 4:
-            r = pltpu.roll(jnp.broadcast_to(r, (8, 128)), 64, 1)[0:1]
         ms[i // 4, pl.ds(i % 4, 1)] = r
     mine = x * 2 + lo
     for peer in near:
@@ -291,7 +345,7 @@
     relay(1)
     relay(0)
     fh[...] = gathered(1)
-    go(fh, fr, f_send.at[0], f_recv.at[0], opposite)
+    go(fh, fr, f_send.at[0], f_recv.at[0], dev(z=z2))
     total = gathered(0)
     landed(fr, f_send.at[0], f_recv.at[0])
     total = total + fr[...]
@@ -348,10 +402,10 @@
     for copy in started:
         copy.wait_send()
     everything = dev(c=1 - c)
-    remote(cu.at[pl.ds(8, 8)], cu.at[pl.ds(8, 8)], b_send.at[0], b_recv.at[0], everything).wait_send()
-    for zs in range(4):
-        all7 = tr.at[zs, pl.ds(0, 7)]
-        remote(all7, all7, t_send.at[zs], t_recv.at[zs], everything).wait_send()
+    for g in range(GROUPS):
+        for side in (0, 1):
+            all7 = tr.at[g, side, pl.ds(0, 7)]
+            remote(all7, all7, t_send.at[g, side], t_recv.at[g, side], everything).wait_send()
     m15 = mr.at[pl.ds(0, 15)]
     remote(m15, m15, m_send, m_recv, everything).wait_send()
     put.wait()
@@ -375,12 +429,12 @@
         scratch_shapes=[
             vmem((ROWS, D), bf16),
             vmem((512, D), bf16),
-            vmem((GROUPS, 4, 2, 128, D), bf16),
+            vmem((GROUPS, 4, 2, 2, 64, D), bf16),
             vmem((16, PIECE, D), bf16),
             vmem((8, 128), f32),
             vmem((8, 128, 128), f32),
             vmem((4, 4, 1024, 256), f32),
-            vmem((4, 8, 4, 1, 256), f32),
+            vmem((GROUPS, 2, 8, 2, 1, 256), f32),
             vmem((16, PIECE, D), f32),
             vmem((16, PIECE, D), bf16),
             vmem((8, 128, 128), f32),
@@ -395,9 +449,9 @@
             vmem((2, 4, 128), f32),
             dma((2,)),
             dma((GROUPS, 6)), dma((GROUPS, 6)),
-            dma((GROUPS, 4)), dma((GROUPS, 4)),
-            dma((2,)), dma((2,)),
-            dma((4,)), dma((4,)),
+            dma((GROUPS, 8)), dma((GROUPS, 8)),
+            dma((9,)), dma((9,)),
+            dma((GROUPS, 2)), dma((GROUPS, 2)),
             dma((2, 5)), dma((2, 5)),
             dma((2, 2)), dma((2, 2)),
             dma((1,)), dma((1,)),

time: 87.4 us -> 82.7 us (0.946); the launches traced: 86 us -> 82.5 us
  Pallas kernels: 81.4 us -> 78 us
    pallas_call x1, Pallas kernels: 81.4 us -> 78 us  [local(): pl.pallas_call(body, out_shape=(jax.ShapeDtypeStruct((2, 4, 2, PIECE, D),...]
where the time goes in v3:
time: 82.7 us; the launch traced here: 82.5 us
  Pallas kernels  78 us (94%)
  other arithmetic  3.31 us (4%)
    pallas_call x1, Pallas kernels, local(): pl.pallas_call(body, out_shape=(jax.ShapeDtypeStruct((2, 4, 2, PIECE, D),...  78 us
    convert_element_type x1, other arithmetic, local(): return (made.reshape(1024, D).astype(f32), weights.reshape(1024))  3.31 us

profile of v3, /device:TPU:25, one launch (start us, length us, event | category | flops | bytes accessed | tf_op | source)
XLA Modules:
  0.0 82.5 jit_solution(6291615924192602385)
XLA Ops:
  0.6 78.0 %em_step.1 = (bf16[2,4,2,64,768]{4,3,2,1,0:T(8,128)(2,1)}, f32[2,4,128]{2,1,0:T(4,128)}) custom-call(bf16[512,768]{1,0:T(8,128)(2,1)} %refs_0_.1, bf16[1024,768]{1,0:T(8,128)(2,1)} %refs_1_.1, f32[8,128]{1,0:T(8,128)} %bitcast.6), custom_call_target="tpu_custom_call" | custom-call | flops 12999999488 | bytes 10000000 | tf_op jit(solution)/shard_map/em_step/pallas_call | solution.py:421
  78.6 0.0 copy-start
  78.6 3.3 %bitcast_convert_fusion = f32[1024,768]{1,0:T(8,128)} fusion(bf16[2,4,2,64,768]{4,3,2,1,0:T(8,128)(2,1)} %get-tuple-element.4), kind=kLoop, calls=%fused_computation | loop fusion | flops 786432 | bytes 4718592 | tf_op jit(solution)/shard_map/convert_element_type | solution.py:470
  81.9 0.0 copy-done
  81.9 0.6 copy.6
Async XLA Ops:
  78.6 3.3 %copy-start = (f32[2,4,128]{2,1,0:T(4,128)S(1)}, f32[2,4,128]{2,1,0:T(4,128)}, u32[]{:S(2)}) copy-start(f32[2,4,128]{2,1,0:T(4,128)} %get-tuple-element.5) | copy-start | bytes 12292

commit v4 on v3

--- a/solution.py
+++ b/solution.py
@@ -71,7 +71,8 @@
     near = [dev(lo=1 - lo)] + [dev(x=xx, lo=ll) for xx in (xp, xm, x2) for ll in (0, 1)]
     across = [dev(z=z2, x=xx, lo=ll) for xx in range(4) for ll in (0, 1)]
     barrier = pltpu.get_barrier_semaphore()
-    for peer in line + near + across:
+    greeted = [twin_core, dev(z=zp), dev(z=zm), dev(z=z2), dev(hi=1 - hi, lo=1 - lo)] + near[:5]
+    for peer in greeted:
         pl.semaphore_signal(barrier, inc=1, device_id=peer, device_id_type=MESH)
 
     get_x.wait()
@@ -84,28 +85,15 @@
 
     lax.fori_loop(0, ROWS // 64, unit_rows, 0)
     get_c.wait()
-
-    def unit_centroids(i, _):
-        cu[i] = unit(cr[pl.ds(pl.multiple_of(i * 64, 64), 64)])
-        return 0
-
-    lax.fori_loop(0, 8, unit_centroids, 0)
+    here = x * 2 + lo
+    cu[here] = unit(cr[pl.ds(pl.multiple_of(here * 64, 64), 64)])
 
     def offsets(i, ref, base):
         r = ref[pl.ds(c * 4 + i, 1), :]
         wide = jnp.broadcast_to(r, (128, 128))
         lmc[base + i] = (wide.T - CONCENTRATION) * LOG2E
 
-    for i in range(4):
-        offsets(i, lm, 0)
-
-    def clear(i, _):
-        ps[i] = jnp.zeros((PIECE, D), jnp.float32)
-        return 0
-
-    lax.fori_loop(0, 16, clear, 0)
-    ma[...] = jnp.zeros_like(ma)
-    pl.semaphore_wait(barrier, len(line + near + across))
+    pl.semaphore_wait(barrier, len(greeted))
 
     up, down = (z % 2) * 2, ((z + 1) % 2) * 2 + 1
     from_up, from_down = (z % 2) * 2 + 1, ((z + 1) % 2) * 2
@@ -165,7 +153,6 @@
         landed(cu.at[8 + xx * 2 + ll], b_send.at[0], b_recv.at[recv])
 
     across_out(0)
-    here = x * 2 + lo
     go(cu.at[here], cu.at[8 + here], b_send.at[7], b_recv.at[7], dev(z=z2))
     go(lm, lmh, b_send.at[8], b_recv.at[8], dev(z=z2))
     along_out(0)
@@ -246,6 +233,24 @@
 
         lax.fori_loop(begin, end, body, 0, unroll=2)
 
+    def unit_centroids(i, _):
+        @pl.when(i != here)
+        def _():
+            cu[i] = unit(cr[pl.ds(pl.multiple_of(i * 64, 64), 64)])
+
+        return 0
+
+    lax.fori_loop(0, 8, unit_centroids, 0)
+
+    for i in range(4):
+        offsets(i, lm, 0)
+
+    def clear(i, _):
+        ps[i] = jnp.zeros((PIECE, D), jnp.float32)
+        return 0
+
+    lax.fori_loop(0, 16, clear, 0)
+    ma[...] = jnp.zeros_like(ma)
     relay_rows(0)
     along_out(2)
     slices_out()
@@ -260,8 +265,10 @@
     scores(0, 0)
     far_rows(1)
     relay_rows(3)
+    near_rows(2)
+    near_rows(3)
+    far_rows(2)
     slices_in()
-    near_rows(2)
     landed(lmh, b_send.at[8], b_recv.at[8])
     for i in range(4):
         offsets(i, lmh, 4)
@@ -271,15 +278,13 @@
     scores(1, 0)
     scores(1, 1)
     totals_out(1)
-    far_rows(2)
-    near_rows(3)
-    totals_in(0)
-    weigh(0, 0, 4)
-    far_rows(3)
     shared(2)
     scores(2, 0)
     scores(2, 1)
     totals_out(2)
+    far_rows(3)
+    totals_in(0)
+    weigh(0, 0, 4)
     shared(3)
     scores(3, 0)
     scores(3, 1)
@@ -385,18 +390,28 @@
     twin(xp, 0, 4)
     handed(x, 1 - lo, 0)
     twin(x, 1 - lo, 5)
-    handed(x2, 0, 5)
-    twin(x2, 0, 6)
-    handed(x2, 1, 6)
-    twin(x2, 1, 7)
-    for k, (xx, ll) in enumerate(
-        ((x, lo), (xm, 0), (xp, 1), (xm, 1), (xp, 0), (x, 1 - lo), (x2, 0), (x2, 1))
-    ):
+    pieces = ((x, lo), (xm, 0), (xp, 1), (xm, 1), (xp, 0), (x, 1 - lo), (x2, 0), (x2, 1))
+    puts = []
+
+    def put_piece(plane, xx, ll):
+        put = pltpu.make_async_copy(ob.at[plane, xx, ll], out.at[plane, xx, ll], out_sem.at[1 + len(puts)])
+        put.start()
+        puts.append(put)
+
+    for xx, ll in pieces[:6]:
+        put_piece(c, xx, ll)
+    for k, (xx, ll) in enumerate(pieces[:6]):
         landed(ob.at[1 - c, xx, ll], q_send.at[k], q_recv.at[k])
+        put_piece(1 - c, xx, ll)
+    for k in (6, 7):
+        handed(x2, k - 6, k - 1)
+        twin(x2, k - 6, k)
+        put_piece(c, x2, k - 6)
+    for k in (6, 7):
+        landed(ob.at[1 - c, x2, k - 6], q_send.at[k], q_recv.at[k])
+        put_piece(1 - c, x2, k - 6)
     landed(wo.at[1 - c], w_send.at[0], w_recv.at[0])
-    put = pltpu.make_async_copy(ob, out, out_sem.at[0])
-    put.start()
-    put_w = pltpu.make_async_copy(wo, wout, out_sem.at[1])
+    put_w = pltpu.make_async_copy(wo, wout, out_sem.at[0])
     put_w.start()
 
     for copy in started:
@@ -408,7 +423,8 @@
             remote(all7, all7, t_send.at[g, side], t_recv.at[g, side], everything).wait_send()
     m15 = mr.at[pl.ds(0, 15)]
     remote(m15, m15, m_send, m_recv, everything).wait_send()
-    put.wait()
+    for put in puts:
+        put.wait()
     put_w.wait()
 
 
@@ -459,7 +475,7 @@
             dma((7,)), dma((7,)),
             dma((8,)), dma((8,)),
             dma((1,)), dma((1,)),
-            dma((2,)),
+            dma((17,)),
         ],
         compiler_params=pltpu.CompilerParams(
             collective_id=0, has_side_effects=True, vmem_limit_bytes=60 * 1024 * 1024

time: 82.7 us -> 79.7 us (0.964)
  Pallas kernels: 78 us -> 74.9 us
    pallas_call x1, Pallas kernels: 78 us -> 74.9 us  [local(): pl.pallas_call(body, out_shape=(jax.ShapeDtypeStruct((2, 4, 2, PIECE, D),...]
where the time goes in v4:
time: 79.7 us; the launch traced here: 79.4 us
  Pallas kernels  74.9 us (94%)
  other arithmetic  3.31 us (4%)
    pallas_call x1, Pallas kernels, local(): pl.pallas_call(body, out_shape=(jax.ShapeDtypeStruct((2, 4, 2, PIECE, D),...  74.9 us
    convert_element_type x1, other arithmetic, local(): return (made.reshape(1024, D).astype(f32), weights.reshape(1024))  3.31 us

profile of v4, /device:TPU:25, one launch (start us, length us, event | category | flops | bytes accessed | tf_op | source)
XLA Modules:
  0.0 79.4 jit_solution(3039126492412366841)
XLA Ops:
  0.6 74.9 %em_step.1 = (bf16[2,4,2,64,768]{4,3,2,1,0:T(8,128)(2,1)}, f32[2,4,128]{2,1,0:T(4,128)}) custom-call(bf16[512,768]{1,0:T(8,128)(2,1)} %refs_0_.1, bf16[1024,768]{1,0:T(8,128)(2,1)} %refs_1_.1, f32[8,128]{1,0:T(8,128)} %bitcast.6), custom_call_target="tpu_custom_call" | custom-call | flops 12999999488 | bytes 10000000 | tf_op jit(solution)/shard_map/em_step/pallas_call | solution.py:437
  75.5 0.0 copy-start
  75.5 3.3 %bitcast_convert_fusion = f32[1024,768]{1,0:T(8,128)} fusion(bf16[2,4,2,64,768]{4,3,2,1,0:T(8,128)(2,1)} %get-tuple-element.4), kind=kLoop, calls=%fused_computation | loop fusion | flops 786432 | bytes 4718592 | tf_op jit(solution)/shard_map/convert_element_type | solution.py:486
  78.8 0.0 copy-done
  78.8 0.6 copy.6
Async XLA Ops:
  75.5 3.3 %copy-start = (f32[2,4,128]{2,1,0:T(4,128)S(1)}, f32[2,4,128]{2,1,0:T(4,128)}, u32[]{:S(2)}) copy-start(f32[2,4,128]{2,1,0:T(4,128)} %get-tuple-element.5) | copy-start | bytes 12292

commit v5 on v4

--- a/solution.py
+++ b/solution.py
@@ -304,12 +304,15 @@
 
     def scatter(ch):
         base = ch * 8
+        go(pb.at[base + x2 * 2], ra.at[ch, 0], r_send.at[ch, 0], r_recv.at[ch, 0], dev(x=xp))
+        go(pb.at[base + x2 * 2 + 1], ra.at[ch, 1], r_send.at[ch, 1], r_recv.at[ch, 1], dev(x=xm))
+
+    def scatter_direct(ch):
+        base = ch * 8
 
         def send(k, src, slot, to):
             go(src, rc.at[ch, slot], c_send.at[ch, k], c_recv.at[ch, slot], to)
 
-        go(pb.at[base + x2 * 2], ra.at[ch, 0], r_send.at[ch, 0], r_recv.at[ch, 0], dev(x=xp))
-        go(pb.at[base + x2 * 2 + 1], ra.at[ch, 1], r_send.at[ch, 1], r_recv.at[ch, 1], dev(x=xm))
         send(0, pb.at[base + xp * 2 + 1], lo, dev(x=xp, lo=1))
         send(1, pb.at[base + xm * 2], 2 + lo, dev(x=xm, lo=0))
         send(2, pb.at[base + x * 2 + 1 - lo], 4, dev(lo=1 - lo))
@@ -333,10 +336,16 @@
     weigh(3, 2, 4)
     pack(1)
     scatter(1)
+    scatter_direct(1)
     weigh(3, 0, 2)
     pack(0)
     scatter(0)
 
+    relay(1)
+    scatter_direct(0)
+    relay(0)
+    fh[...] = gathered(1)
+    go(fh, fr, f_send.at[0], f_recv.at[0], dev(z=z2))
     for i in range(8):
         r = jnp.sum(ma[i].T, axis=0, keepdims=True)
         ms[i // 4, pl.ds(i % 4, 1)] = r
@@ -347,10 +356,6 @@
         remote(ms.at[1], mr.at[8 + mine], m_send, m_recv, peer).start()
     mr[mine] = ms[0]
 
-    relay(1)
-    relay(0)
-    fh[...] = gathered(1)
-    go(fh, fr, f_send.at[0], f_recv.at[0], dev(z=z2))
     total = gathered(0)
     landed(fr, f_send.at[0], f_recv.at[0])
     total = total + fr[...]

time: 79.7 us -> 77.5 us (0.972)
  Pallas kernels: 74.9 us -> 72.7 us
    pallas_call x1, Pallas kernels: 74.9 us -> 72.7 us  [local(): pl.pallas_call(body, out_shape=(jax.ShapeDtypeStruct((2, 4, 2, PIECE, D),...]
where the time goes in v5:
time: 77.5 us; the launch traced here: 77.3 us
  Pallas kernels  72.7 us (94%)
  other arithmetic  3.31 us (4%)
    pallas_call x1, Pallas kernels, local(): pl.pallas_call(body, out_shape=(jax.ShapeDtypeStruct((2, 4, 2, PIECE, D),...  72.7 us
    convert_element_type x1, other arithmetic, local(): return (made.reshape(1024, D).astype(f32), weights.reshape(1024))  3.31 us

profile of v5, /device:TPU:25, one launch (start us, length us, event | category | flops | bytes accessed | tf_op | source)
XLA Modules:
  0.0 77.3 jit_solution(11271673486003716130)
XLA Ops:
  0.6 72.7 %em_step.1 = (bf16[2,4,2,64,768]{4,3,2,1,0:T(8,128)(2,1)}, f32[2,4,128]{2,1,0:T(4,128)}) custom-call(bf16[512,768]{1,0:T(8,128)(2,1)} %refs_0_.1, bf16[1024,768]{1,0:T(8,128)(2,1)} %refs_1_.1, f32[8,128]{1,0:T(8,128)} %bitcast.6), custom_call_target="tpu_custom_call" | custom-call | flops 12999999488 | bytes 10000000 | tf_op jit(solution)/shard_map/em_step/pallas_call | solution.py:442
  73.4 0.0 copy-start
  73.4 3.3 %bitcast_convert_fusion = f32[1024,768]{1,0:T(8,128)} fusion(bf16[2,4,2,64,768]{4,3,2,1,0:T(8,128)(2,1)} %get-tuple-element.4), kind=kLoop, calls=%fused_computation | loop fusion | flops 786432 | bytes 4718592 | tf_op jit(solution)/shard_map/convert_element_type | solution.py:491
  76.7 0.0 copy-done
  76.7 0.6 copy.6
Async XLA Ops:
  73.4 3.3 %copy-start = (f32[2,4,128]{2,1,0:T(4,128)S(1)}, f32[2,4,128]{2,1,0:T(4,128)}, u32[]{:S(2)}) copy-start(f32[2,4,128]{2,1,0:T(4,128)} %get-tuple-element.5) | copy-start | bytes 12292

commit v6 on v5

--- a/solution.py
+++ b/solution.py
@@ -379,10 +379,6 @@
     hand(x, lo, 4, 0, dev(lo=1 - lo))
     twin(x, lo, 0)
 
-    landed(mr.at[pl.ds(0, 15)], m_send, m_recv)
-    wo[c] = jnp.sum(mr[...], axis=0) * factor
-    go(wo.at[c], wo.at[c], w_send.at[0], w_recv.at[0], dev(c=1 - c))
-
     handed(xm, 0, 1)
     hand(xm, 0, 5, 5, dev(x=xp))
     handed(xp, 1, 4)
@@ -395,6 +391,10 @@
     twin(xp, 0, 4)
     handed(x, 1 - lo, 0)
     twin(x, 1 - lo, 5)
+
+    landed(mr.at[pl.ds(0, 15)], m_send, m_recv)
+    wo[c] = jnp.sum(mr[...], axis=0) * factor
+    go(wo.at[c], wo.at[c], w_send.at[0], w_recv.at[0], dev(c=1 - c))
     pieces = ((x, lo), (xm, 0), (xp, 1), (xm, 1), (xp, 0), (x, 1 - lo), (x2, 0), (x2, 1))
     puts = []
 

time: 77.5 us -> 77.5 us (level)
  no operation moved by 1% of the time
where the time goes in v6:
time: 77.5 us; the launch traced here: 77.3 us
  Pallas kernels  72.7 us (94%)
  other arithmetic  3.31 us (4%)
    pallas_call x1, Pallas kernels, local(): pl.pallas_call(body, out_shape=(jax.ShapeDtypeStruct((2, 4, 2, PIECE, D),...  72.7 us
    convert_element_type x1, other arithmetic, local(): return (made.reshape(1024, D).astype(f32), weights.reshape(1024))  3.31 us

profile of v6, /device:TPU:25, one launch (start us, length us, event | category | flops | bytes accessed | tf_op | source)
XLA Modules:
  0.0 77.3 jit_solution(18422410074217487829)
XLA Ops:
  0.6 72.7 %em_step.1 = (bf16[2,4,2,64,768]{4,3,2,1,0:T(8,128)(2,1)}, f32[2,4,128]{2,1,0:T(4,128)}) custom-call(bf16[512,768]{1,0:T(8,128)(2,1)} %refs_0_.1, bf16[1024,768]{1,0:T(8,128)(2,1)} %refs_1_.1, f32[8,128]{1,0:T(8,128)} %bitcast.6), custom_call_target="tpu_custom_call" | custom-call | flops 12999999488 | bytes 10000000 | tf_op jit(solution)/shard_map/em_step/pallas_call | solution.py:442
  73.4 0.0 copy-start
  73.4 3.3 %bitcast_convert_fusion = f32[1024,768]{1,0:T(8,128)} fusion(bf16[2,4,2,64,768]{4,3,2,1,0:T(8,128)(2,1)} %get-tuple-element.4), kind=kLoop, calls=%fused_computation | loop fusion | flops 786432 | bytes 4718592 | tf_op jit(solution)/shard_map/convert_element_type | solution.py:491
  76.7 0.0 copy-done
  76.7 0.6 copy.6
Async XLA Ops:
  73.4 3.3 %copy-start = (f32[2,4,128]{2,1,0:T(4,128)S(1)}, f32[2,4,128]{2,1,0:T(4,128)}, u32[]{:S(2)}) copy-start(f32[2,4,128]{2,1,0:T(4,128)} %get-tuple-element.5) | copy-start | bytes 12292
